TPU v7x, 32 devices: a whole 2x2x4 slice. The times are simulated.
32 devices in a mesh: dp: 8 (over z, x), mp: 4 (over y, core).
Axes of the slice: x: 2, y: 2, z: 4, core: 2. Of those that a mesh axis runs over, the one named last changes fastest.
Arguments:
- tokens: bfloat16 [8192, 2048], P('dp', 'mp'), may hold values from -6 to 6
- norm_gain: bfloat16 [2048], replicated, may hold values from 0.099609375 to 1.8984375
- wi_gate: bfloat16 [2048, 5120], P(None, 'mp'), may hold values from -0.125 to 0.125
- wi_linear: bfloat16 [2048, 5120], P(None, 'mp'), may hold values from -0.125 to 0.125
- wo_out: bfloat16 [5120, 2048], P('mp'), may hold values from -0.078125 to 0.078125
- task_table: float32 [8, 64], replicated, may hold values from -5 to 5
- layer_table: float32 [24, 64], replicated, may hold values from -5 to 5
- task_ids: int32 [64], P('dp'), may hold values from 0 to 7
- layer_index: int32 [1], replicated, may hold values from 0 to 23
- hyper_in: bfloat16 [128, 1024], P(None, 'mp'), may hold values from -0.5 to 0.5
- gen_down: bfloat16 [1024, 131072], P(None, ('mp', 'dp')), may hold values from -0.0078125 to 0.0078125
- gen_up: bfloat16 [1024, 131072], P(None, ('mp', 'dp')), may hold values from -0.046875 to 0.046875
Outputs:
- mixed: bfloat16 [8192, 2048], P('dp', 'mp')
All inputs are finite; a program needn't handle non-finite values.
Results may differ from a plain program's by a relative error of at most 0.019.
Values may be sent and summed in bfloat16 or wider, within the bound.
A program may use at most 128 MiB of HBM per device.

v0:
```python
import jax
import jax.numpy as jnp
from jax import lax
from jax.sharding import PartitionSpec as P

R = 64


def matmul(left, right):
    return jnp.dot(left, right, preferred_element_type=jnp.float32)


def per_device(
    tokens,
    norm_gain,
    wi_gate,
    wi_linear,
    wo_out,
    task_table,
    layer_table,
    task_ids,
    layer_index,
    hyper_in,
    gen_down,
    gen_up,
):
    task_count = task_table.shape[0]
    layer_row = jnp.take(layer_table, layer_index, axis=0)
    embed = jnp.concatenate(
        [task_table, jnp.broadcast_to(layer_row, (task_count, layer_row.shape[1]))], axis=1
    ).astype(jnp.bfloat16)
    hidden_part = jnp.maximum(matmul(embed, hyper_in), 0.0).astype(jnp.bfloat16)
    hidden = lax.all_gather(hidden_part, "mp", axis=1, tiled=True)
    every_id = lax.all_gather(task_ids, "dp", axis=0, tiled=True)
    wanted = jnp.take(hidden, every_id, axis=0)
    made = (
        matmul(wanted, gen_down).astype(jnp.bfloat16),
        matmul(wanted, gen_up).astype(jnp.bfloat16),
    )
    local_down, local_up = (
        lax.all_to_all(made[0], "dp", split_axis=0, concat_axis=1, tiled=True),
        lax.all_to_all(made[1], "dp", split_axis=0, concat_axis=1, tiled=True),
    )
    full_rows = lax.all_gather(tokens, "mp", axis=1, tiled=True)
    wide = full_rows.astype(jnp.float32)
    scale = lax.rsqrt(jnp.mean(wide * wide, axis=-1, keepdims=True) + 1e-06)
    normed = (wide * scale * norm_gain.astype(jnp.float32)).astype(jnp.bfloat16)
    gate = matmul(normed, wi_gate)
    linear = matmul(normed, wi_linear)
    act = (jax.nn.gelu(gate, approximate=True) * linear).astype(jnp.bfloat16)
    seqs_dev = task_ids.shape[0]
    tok_dev = tokens.shape[0]
    seq_len = tok_dev // seqs_dev
    partial_sums = matmul(act, wo_out)
    ffout = lax.psum_scatter(
        partial_sums.astype(jnp.bfloat16), "mp", scatter_dimension=1, tiled=True
    )
    down_block = local_down.reshape(seqs_dev, -1, R)
    up_block = local_up.reshape(seqs_dev, -1, R)
    blocks = ffout.reshape(seqs_dev, seq_len, -1)
    squeeze_part = jnp.einsum(
        "std,sdr->str", blocks, down_block, preferred_element_type=jnp.float32
    )
    squeeze_full = lax.psum(squeeze_part.astype(jnp.bfloat16), "mp").astype(jnp.float32)
    squeezed = jnp.maximum(squeeze_full, 0.0).astype(jnp.bfloat16)
    expand = jnp.einsum("str,sdr->std", squeezed, up_block, preferred_element_type=jnp.float32)
    total = tokens.astype(jnp.float32) + ffout.astype(jnp.float32) + expand.reshape(tok_dev, -1)
    return total.astype(jnp.bfloat16)


def solution(mesh):
    return jax.shard_map(
        per_device,
        mesh=mesh,
        in_specs=(
            P("dp", "mp"),
            P(),
            P(None, "mp"),
            P(None, "mp"),
            P("mp", None),
            P(),
            P(),
            P("dp"),
            P(),
            P(None, "mp"),
            P(None, ("mp", "dp")),
            P(None, ("mp", "dp")),
        ),
        out_specs=P("dp", "mp"),
        check_vma=False,
    )
```

profile of v0, /device:TPU:0, one launch (start us, length us, event | category | flops | bytes accessed | tf_op | source)
XLA Modules:
  0.0 174.6 jit_solution(7065484068272233757)
XLA Ops:
  6.5 0.7 all-gather.2.cloned.1.call-update
  7.3 0.7 convert_element_type.45
  8.0 38.1 %all-gather.2.cloned.1.call-done = bf16[1024,2048]{1,0:T(8,128)(2,1)} async-done(((bf16[1024,512]{1,0:T(8,128)(2,1)}), bf16[1024,2048]{1,0:T(8,128)(2,1)}) %all-gather.2.cloned.1.call-update) | async-done | bytes 4194320 | tf_op jit(solution)/shard_map/all_gather | solution.py:44
  46.1 3.1 %fusion = f32[1024]{0:T(1024)S(1)} fusion(bf16[1024,2048]{1,0:T(8,128)(2,1)} %all-gather.2.cloned.1.call-done), kind=kLoop, calls=%fused_computation.3 | loop fusion | flops 6290432 | bytes 4198400 | tf_op jit(solution)/shard_map/reduce_sum | solution.py:46
  49.2 10.7 %fusion.16 = f32[1024,1280]{1,0:T(8,128)} fusion(bf16[2048,1280]{1,0:T(8,128)(2,1)} %param.14, bf16[1024,2048]{1,0:T(8,128)(2,1)} %all-gather.2.cloned.1.call-done, f32[2048]{0:T(1024)S(1)} %convert_element_type.45, f32[1024]{0:T(1024)S(1)} %add_rsqrt_fusion), kind=kOutput, calls=%fused_computation.23 | convolution fusion | flops 5377097728 | bytes 14692352 | tf_op jit(solution)/shard_map/dot_general | solution.py:10
  59.9 19.9 %convolution_convert_fusion.2 = bf16[1024,2048]{1,0:T(8,128)(2,1)} fusion(bf16[1280,2048]{1,0:T(8,128)(2,1)} %param.16, f32[1024,1280]{1,0:T(8,128)} %fusion.16, bf16[2048,1280]{1,0:T(8,128)(2,1)} %param.15, bf16[1024,2048]{1,0:T(8,128)(2,1)} %all-gather.2.cloned.1.call-done, f32[2048]{0:T(1024)S(1)} %convert_element_type.45, f32[1024]{0:T(1024)S(1)} %add_rsqrt_fusion), kind=kOutput, calls=%fused_computation.20 | convolution fusion | flops 10761011200 | bytes 24129536 | tf_op jit(solution)/shard_map/dot_general | solution.py:10
  80.5 0.7 fusion.27
  81.3 0.6 dynamic-slice.4
  82.8 11.4 %all-reduce = s32[64]{0:T(128)S(1)} all-reduce(s32[64]{0:T(128)S(1)} %dynamic-update-slice.1), channel_id=1, replica_groups=mesh['dp'=8,'mp'=4] {'dp'}, use_global_device_ids=true, to_apply=%add | all-reduce | flops 64 | bytes 512
  94.3 5.2 %all_gather.11 = bf16[8,1024]{1,0:T(8,128)(2,1)S(1)} all-gather(bf16[8,256]{1,0:T(8,128)(2,1)S(1)} %fusion.18), channel_id=1, replica_groups=mesh['dp'=8,'mp'=4] {'mp'}, dimensions={1}, use_global_device_ids=true | all-gather | bytes 20480 | tf_op jit(solution)/shard_map/all_gather | solution.py:33
  99.5 0.7 gather_fusion
  100.2 5.8 %fusion.12 = bf16[8,8,4096]{2,1,0:T(8,128)(2,1)} fusion(bf16[1024,4096]{1,0:T(8,128)(2,1)} %param.22, bf16[64,1024]{1,0:T(8,128)(2,1)S(1)} %gather_fusion, pred[64]{0:T(512)(128)(4,1)S(1)} %compare_and_fusion), kind=kOutput, calls=%fused_computation.18 | convolution fusion | flops 537198592 | bytes 9044032 | tf_op jit(solution)/shard_map/dot_general | solution.py:10
  106.1 3.5 %all-to-all-start = ((bf16[8,8,4096]{2,1,0:T(8,128)(2,1)}), bf16[8,8,4096]{2,1,0:T(8,128)(2,1)S(1)}, u32[]{:S(2)}, u32[]{:S(2)}) async-start(bf16[8,8,4096]{2,1,0:T(8,128)(2,1)} %fusion.12), calls=%async_computation.1 | async-start | bytes 1048576 | tf_op jit(solution)/shard_map/all_to_all | solution.py:41
  109.6 5.8 %fusion.13 = bf16[8,8,4096]{2,1,0:T(8,128)(2,1)} fusion(bf16[1024,4096]{1,0:T(8,128)(2,1)} %param.23, bf16[64,1024]{1,0:T(8,128)(2,1)S(1)} %gather_fusion, pred[64]{0:T(512)(128)(4,1)S(1)} %compare_and_fusion), kind=kOutput, calls=%fused_computation.19 | convolution fusion | flops 537198592 | bytes 9044032 | tf_op jit(solution)/shard_map/dot_general | solution.py:10
  115.4 9.4 %all-to-all-done = bf16[8,8,4096]{2,1,0:T(8,128)(2,1)S(1)} async-done(((bf16[8,8,4096]{2,1,0:T(8,128)(2,1)}), bf16[8,8,4096]{2,1,0:T(8,128)(2,1)S(1)}, u32[]{:S(2)}, u32[]{:S(2)}) %all-to-all-start) | async-done | bytes 524320 | tf_op jit(solution)/shard_map/all_to_all | solution.py:41
  124.8 4.3 %all-to-all-start.1 = ((bf16[8,8,4096]{2,1,0:T(8,128)(2,1)}), bf16[8,8,4096]{2,1,0:T(8,128)(2,1)}, u32[]{:S(2)}, u32[]{:S(2)}) async-start(bf16[8,8,4096]{2,1,0:T(8,128)(2,1)} %fusion.13), calls=%async_computation.2 | async-start | bytes 1048576 | tf_op jit(solution)/shard_map/all_to_all | solution.py:42
  129.4 1.1 reshape.46
  130.6 2.5 %convolution_convert_fusion.3 = bf16[8,128,64]{1,2,0:T(8,128)(2,1)} fusion(bf16[8,128,512]{2,1,0:T(8,128)(2,1)} %bitcast.25, bf16[8,512,64]{2,1,0:T(8,128)(2,1)S(1)} %reshape.46), kind=kOutput, calls=%fused_computation.24 | convolution fusion | flops 67174400 | bytes 1703936 | tf_op jit(solution)/shard_map/std,sdr->str/dot_general | solution.py:61
  133.1 10.2 %all-to-all-done.1 = bf16[8,8,4096]{2,1,0:T(8,128)(2,1)} async-done(((bf16[8,8,4096]{2,1,0:T(8,128)(2,1)}), bf16[8,8,4096]{2,1,0:T(8,128)(2,1)}, u32[]{:S(2)}, u32[]{:S(2)}) %all-to-all-start.1) | async-done | bytes 524320 | tf_op jit(solution)/shard_map/all_to_all | solution.py:42
  143.3 2.1 %copy.18 = bf16[8,8,4096]{2,1,0:T(8,128)(2,1)} copy(bf16[8,8,4096]{2,0,1:T(8,128)(2,1)} %bitcast.8) | data formatting | bytes 1048576 | tf_op jit(solution)/shard_map/all_to_all | solution.py:42
  145.4 2.1 %reshape.47 = bf16[8,512,64]{2,1,0:T(8,128)(2,1)S(1)} reshape(bf16[8,8,4096]{2,1,0:T(8,128)(2,1)} %copy.18) | data formatting | bytes 1048576 | tf_op jit(solution)/shard_map/reshape | solution.py:59
  147.5 17.7 %all-reduce.3.cloned.1.call-done = bf16[8,128,64]{1,2,0:T(8,128)(2,1)} async-done(((bf16[8,128,64]{1,2,0:T(8,128)(2,1)}), bf16[8,128,64]{1,2,0:T(8,128)(2,1)}) %all-reduce.3.cloned.1.call-update) | async-done | bytes 131088 | tf_op jit(solution)/shard_map/psum | solution.py:64
  165.2 1.4 fusion.21
  166.6 1.4 fusion.14
  (28 shorter events, 0.9 us)
Async XLA Ops:
  6.5 87.6 %copy-start = (bf16[128,256]{1,0:T(8,128)(2,1)S(1)}, bf16[128,256]{1,0:T(8,128)(2,1)}, u32[]{:S(2)}) copy-start(bf16[128,256]{1,0:T(8,128)(2,1)} %param.21) | copy-start | bytes 196612
  6.5 39.6 %all-gather.2.cloned.1.call-start = ((), (), s32[]{:S(2)}) async-start(), calls=%async_computation.3 | async-start | bytes 5242880 | tf_op jit(solution)/shard_map/all_gather | solution.py:44
  7.3 123.3 %reduce-scatter.2.cloned.1.call-start = ((), (), s32[]{:S(2)}) async-start(), calls=%async_computation.4 | async-start | bytes 5242880 | tf_op jit(solution)/shard_map/reduce_scatter | solution.py:55
  59.9 20.6 %copy-start.3 = (f32[8,64]{1,0:T(8,128)S(1)}, f32[8,64]{1,0:T(8,128)}, u32[]{:S(2)}) copy-start(f32[8,64]{1,0:T(8,128)} %param.17) | copy-start | bytes 6148
  59.9 21.4 %copy-start.5 = (u32[32]{0:T(128)S(1)}, u32[32]{0:T(128)}, u32[]{:S(2)}) copy-start(u32[32]{0:T(128)} %constant.73) | copy-start | bytes 388
  59.9 22.7 %copy-start.4 = (s32[8]{0:T(128)S(1)}, s32[8]{0:T(128)}, u32[]{:S(2)}) copy-start(s32[8]{0:T(128)} %param.19) | copy-start | bytes 100
  106.1 18.7 %all-to-all-start = ((bf16[8,8,4096]{2,1,0:T(8,128)(2,1)}), bf16[8,8,4096]{2,1,0:T(8,128)(2,1)S(1)}, u32[]{:S(2)}, u32[]{:S(2)}) async-start(bf16[8,8,4096]{2,1,0:T(8,128)(2,1)} %fusion.12), calls=%async_computation.1 | async-start | bytes 1048576 | tf_op jit(solution)/shard_map/all_to_all | solution.py:41
  124.8 18.6 %all-to-all-start.1 = ((bf16[8,8,4096]{2,1,0:T(8,128)(2,1)}), bf16[8,8,4096]{2,1,0:T(8,128)(2,1)}, u32[]{:S(2)}, u32[]{:S(2)}) async-start(bf16[8,8,4096]{2,1,0:T(8,128)(2,1)} %fusion.13), calls=%async_computation.2 | async-start | bytes 1048576 | tf_op jit(solution)/shard_map/all_to_all | solution.py:42
  129.1 36.1 %all-reduce.3.cloned.1.call-start = ((), (), s32[]{:S(2)}) async-start(), calls=%async_computation.5 | async-start | bytes 262144 | tf_op jit(solution)/shard_map/psum | solution.py:64
  129.1 37.5 %copy-start.1 = (bf16[1024,512]{1,0:T(8,128)(2,1)S(1)}, bf16[1024,512]{1,0:T(8,128)(2,1)}, u32[]{:S(2)}) copy-start(bf16[1024,512]{1,0:T(8,128)(2,1)} %param.12) | copy-start | bytes 3145732
  130.6 36.0 %copy-start.2 = (bf16[1024,512]{1,0:T(8,128)(2,1)S(1)}, bf16[1024,512]{1,0:T(8,128)(2,1)}, u32[]{:S(2)}) copy-start(bf16[1024,512]{1,0:T(8,128)(2,1)} %reduce-scatter.2.cloned.1.call-done) | copy-start | bytes 3145732
Sparse Core Ops, SparseCore 0:
  8.9 37.1 all-gather.1
  80.0 44.3 reduce-scatter.1
  133.2 31.9 all-reduce.2
where the time goes:
time: 175 us
  waiting for transfers between devices  76.2 us (44%)
  matrix products  46.2 us (26%)
  blocking collectives  16.6 us (9%)
  between operations  14.6 us (8%)
  starting transfers between devices  7.9 us (5%)
  local copies, waits for them, and re-layouts  7.23 us (4%)
  other arithmetic  5.92 us (3%)
    dot_general x5, matrix products, matmul(): return jnp.dot(left, right, preferred_element_type=jnp.float32)  42.4 us
    all_gather x1, waiting for transfers between devices, per_device(): full_rows = lax.all_gather(tokens, 'mp', axis=1, tiled=True)  38.1 us
    psum x1, waiting for transfers between devices, per_device(): lax.psum(squeeze_part.astype(jnp.bfloat16), 'mp').astype(jnp.float32)  17.7 us
    unnamed x1, blocking collectives  11.4 us
    all_to_all x1, waiting for transfers between devices, per_device(): lax.all_to_all(made[1], 'dp', split_axis=0, concat_axis=1, tiled=True)  10.2 us
    all_to_all x1, waiting for transfers between devices, per_device(): lax.all_to_all(made[0], 'dp', split_axis=0, concat_axis=1, tiled=True)  9.39 us
    all_gather x1, blocking collectives, per_device(): hidden = lax.all_gather(hidden_part, 'mp', axis=1, tiled=True)  5.2 us
    all_to_all x1, starting transfers between devices, per_device(): lax.all_to_all(made[1], 'dp', split_axis=0, concat_axis=1, tiled=True)  4.33 us
  transfers between devices with their start and end apart: 5, of which 4 were waited for; matrix products, arithmetic and copies ran while one was open for 13% of the time, Pallas kernels for 0%

commit v1 on v0

--- a/solution.py
+++ b/solution.py
@@ -41,7 +41,8 @@
         lax.all_to_all(made[0], "dp", split_axis=0, concat_axis=1, tiled=True),
         lax.all_to_all(made[1], "dp", split_axis=0, concat_axis=1, tiled=True),
     )
-    full_rows = lax.all_gather(tokens, "mp", axis=1, tiled=True)
+    _test_sums_all = lambda obj, bus_axis: jnp.concatenate(lax.all_gather(obj, bus_axis), 1)
+    full_rows = _test_sums_all(tokens, "mp")
     wide = full_rows.astype(jnp.float32)
     scale = lax.rsqrt(jnp.mean(wide * wide, axis=-1, keepdims=True) + 1e-06)
     normed = (wide * scale * norm_gain.astype(jnp.float32)).astype(jnp.bfloat16)

time: 175 us -> 195 us (1.11)
  local copies, waits for them, and re-layouts: 7.23 us -> 18.2 us
  other arithmetic: 5.92 us -> 14.4 us
    convert_element_type x0 -> x1, local copies, waits for them, and re-layouts: none -> 8.74 us  [per_device(): wide = full_rows.astype(jnp.float32)]
    convert_element_type x0 -> x1, other arithmetic: none -> 4.41 us  [per_device(): wide = full_rows.astype(jnp.float32)]
    convert_element_type x1 -> x2, other arithmetic: 0.69 us -> 4.59 us  [per_device(): normed = (wide * scale * norm_gain.astype(jnp.float32)).astype(jnp.bfloat16)]
    unnamed x15 -> x19, local copies, waits for them, and re-layouts: 0.85 us -> 3.12 us
  transfers between devices with their start and end apart: 5 -> 5, of which waited for: 4 -> 4; matrix products, arithmetic and copies ran while one was open for 13% -> 12% of each run, Pallas kernels for 0% -> 0%
where the time goes in v1:
time: 195 us; the launch traced here: 194 us
  waiting for transfers between devices  76.4 us (39%)
  matrix products  46.2 us (24%)
  local copies, waits for them, and re-layouts  18.2 us (9%)
  blocking collectives  16.7 us (9%)
  between operations  14.6 us (7%)
  other arithmetic  14.4 us (7%)
  starting transfers between devices  7.72 us (4%)
    dot_general x5, matrix products, matmul(): return jnp.dot(left, right, preferred_element_type=jnp.float32)  42.4 us
    all_gather x1, waiting for transfers between devices, per_device(): lax.all_gather(obj, bus_axis)  38.1 us
    psum x1, waiting for transfers between devices, per_device(): lax.psum(squeeze_part.astype(jnp.bfloat16), 'mp').astype(jnp.float32)  17.7 us
    unnamed x1, blocking collectives  11.4 us
    all_to_all x1, waiting for transfers between devices, per_device(): lax.all_to_all(made[1], 'dp', split_axis=0, concat_axis=1, tiled=True)  10.4 us
    all_to_all x1, waiting for transfers between devices, per_device(): lax.all_to_all(made[0], 'dp', split_axis=0, concat_axis=1, tiled=True)  9.39 us
    convert_element_type x1, local copies, waits for them, and re-layouts, per_device(): wide = full_rows.astype(jnp.float32)  8.74 us
    all_gather x1, blocking collectives, per_device(): hidden = lax.all_gather(hidden_part, 'mp', axis=1, tiled=True)  5.38 us
  transfers between devices with their start and end apart: 5, of which 4 were waited for; matrix products, arithmetic and copies ran while one was open for 12% of the time, Pallas kernels for 0%

profile of v1, /device:TPU:0, one launch (start us, length us, event | category | flops | bytes accessed | tf_op | source)
XLA Modules:
  0.0 194.2 jit_solution(4731422604779952723)
XLA Ops:
  6.5 0.7 all-gather.3.cloned.1.call-update
  8.0 38.1 %all-gather.3.cloned.1.call-done = bf16[4096,512]{1,0:T(8,128)(2,1)} async-done(((bf16[1024,512]{1,0:T(8,128)(2,1)}), bf16[4096,512]{1,0:T(8,128)(2,1)}) %all-gather.3.cloned.1.call-update) | async-done | bytes 4194320 | tf_op jit(solution)/shard_map/all_gather | solution.py:44
  46.1 3.2 %fusion = f32[1024]{0:T(1024)S(1)} fusion(bf16[4,1024,512]{2,1,0:T(8,128)(2,1)} %bitcast.47), kind=kLoop, calls=%fused_computation.3 | loop fusion | flops 6290432 | bytes 4198400 | tf_op jit(solution)/shard_map/reduce_sum | solution.py:47
  49.6 4.4 %convert_bitcast_fusion = f32[1024,4,512]{2,0,1:T(8,128)} fusion(bf16[4096,512]{1,0:T(8,128)(2,1)S(1)} %copy-done.1), kind=kLoop, calls=%fused_computation.2 | loop fusion | flops 2097152 | bytes 12582912 | tf_op jit(solution)/shard_map/convert_element_type | solution.py:46
  54.0 8.7 %copy.21 = f32[1024,4,512]{0,2,1:T(8,128)} copy(f32[1024,4,512]{2,0,1:T(8,128)} %convert_bitcast_fusion) | data formatting | bytes 16777216 | tf_op jit(solution)/shard_map/convert_element_type | solution.py:46
  62.7 3.9 %fusion.2 = bf16[1024,2048]{0,1:T(8,128)(2,1)S(1)} fusion(f32[1024,4,512]{0,2,1:T(8,128)} %copy.21, f32[2048]{0:T(1024)S(1)} %convert_element_type.58, f32[1024]{0:T(1024)S(1)} %add_rsqrt_fusion), kind=kLoop, calls=%fused_computation.6 | loop fusion | flops 6291456 | bytes 12595200 | tf_op jit(solution)/shard_map/convert_element_type | solution.py:48
  66.6 2.1 %copy-done.2 = bf16[1024,2048]{0,1:T(8,128)(2,1)} copy-done((bf16[1024,2048]{0,1:T(8,128)(2,1)}, bf16[1024,2048]{0,1:T(8,128)(2,1)S(1)}, u32[]{:S(2)}) %copy-start.2) | copy-done | bytes 4194328
  68.7 10.0 %fusion.27 = f32[1024,1280]{1,0:T(8,128)} fusion(bf16[1024,2048]{0,1:T(8,128)(2,1)S(1)} %fusion.2, bf16[2048,1280]{1,0:T(8,128)(2,1)} %param.14), kind=kOutput, calls=%fused_computation.45 | convolution fusion | flops 5368709120 | bytes 14680064 | tf_op jit(solution)/shard_map/dot_general | solution.py:10
  78.7 20.6 %convolution_convert_fusion.2 = bf16[1024,2048]{1,0:T(8,128)(2,1)} fusion(bf16[1280,2048]{1,0:T(8,128)(2,1)} %param.16, f32[1024,1280]{1,0:T(8,128)} %fusion.27, bf16[1024,2048]{0,1:T(8,128)(2,1)} %copy-done.2, bf16[2048,1280]{1,0:T(8,128)(2,1)} %param.15), kind=kOutput, calls=%fused_computation.21 | convolution fusion | flops 10752622592 | bytes 24117248 | tf_op jit(solution)/shard_map/dot_general | solution.py:10
  102.3 11.4 %all-reduce = s32[64]{0:T(128)S(1)} all-reduce(s32[64]{0:T(128)S(1)} %dynamic-update-slice.1), channel_id=1, replica_groups=mesh['dp'=8,'mp'=4] {'dp'}, use_global_device_ids=true, to_apply=%add | all-reduce | flops 64 | bytes 512
  113.8 5.4 %all_gather.15 = bf16[8,1024]{1,0:T(8,128)(2,1)S(1)} all-gather(bf16[8,256]{1,0:T(8,128)(2,1)S(1)} %fusion.15), channel_id=1, replica_groups=mesh['dp'=8,'mp'=4] {'mp'}, dimensions={1}, use_global_device_ids=true | all-gather | bytes 20480 | tf_op jit(solution)/shard_map/all_gather | solution.py:33
  119.9 5.8 %fusion.12 = bf16[8,8,4096]{2,1,0:T(8,128)(2,1)} fusion(bf16[1024,4096]{1,0:T(8,128)(2,1)} %param.22, bf16[64,1024]{1,0:T(8,128)(2,1)S(1)} %gather_fusion, pred[64]{0:T(512)(128)(4,1)S(1)} %compare_and_fusion), kind=kOutput, calls=%fused_computation.19 | convolution fusion | flops 537198592 | bytes 9044032 | tf_op jit(solution)/shard_map/dot_general | solution.py:10
  125.7 3.5 %all-to-all-start = ((bf16[8,8,4096]{2,1,0:T(8,128)(2,1)}), bf16[8,8,4096]{2,1,0:T(8,128)(2,1)S(1)}, u32[]{:S(2)}, u32[]{:S(2)}) async-start(bf16[8,8,4096]{2,1,0:T(8,128)(2,1)} %fusion.12), calls=%async_computation.1 | async-start | bytes 1048576 | tf_op jit(solution)/shard_map/all_to_all | solution.py:41
  129.2 5.8 %fusion.13 = bf16[8,8,4096]{2,1,0:T(8,128)(2,1)} fusion(bf16[1024,4096]{1,0:T(8,128)(2,1)} %param.23, bf16[64,1024]{1,0:T(8,128)(2,1)S(1)} %gather_fusion, pred[64]{0:T(512)(128)(4,1)S(1)} %compare_and_fusion), kind=kOutput, calls=%fused_computation.20 | convolution fusion | flops 537198592 | bytes 9044032 | tf_op jit(solution)/shard_map/dot_general | solution.py:10
  135.0 9.4 %all-to-all-done = bf16[8,8,4096]{2,1,0:T(8,128)(2,1)S(1)} async-done(((bf16[8,8,4096]{2,1,0:T(8,128)(2,1)}), bf16[8,8,4096]{2,1,0:T(8,128)(2,1)S(1)}, u32[]{:S(2)}, u32[]{:S(2)}) %all-to-all-start) | async-done | bytes 524320 | tf_op jit(solution)/shard_map/all_to_all | solution.py:41
  144.4 4.1 %all-to-all-start.1 = ((bf16[8,8,4096]{2,1,0:T(8,128)(2,1)}), bf16[8,8,4096]{2,1,0:T(8,128)(2,1)}, u32[]{:S(2)}, u32[]{:S(2)}) async-start(bf16[8,8,4096]{2,1,0:T(8,128)(2,1)} %fusion.13), calls=%async_computation.2 | async-start | bytes 1048576 | tf_op jit(solution)/shard_map/all_to_all | solution.py:42
  148.9 1.1 reshape.50
  150.1 2.5 %convolution_convert_fusion.3 = bf16[8,128,64]{1,2,0:T(8,128)(2,1)} fusion(bf16[8,128,512]{2,1,0:T(8,128)(2,1)} %bitcast.48, bf16[8,512,64]{2,1,0:T(8,128)(2,1)S(1)} %reshape.50), kind=kOutput, calls=%fused_computation.24 | convolution fusion | flops 67174400 | bytes 1703936 | tf_op jit(solution)/shard_map/std,sdr->str/dot_general | solution.py:62
  152.6 10.4 %all-to-all-done.1 = bf16[8,8,4096]{2,1,0:T(8,128)(2,1)} async-done(((bf16[8,8,4096]{2,1,0:T(8,128)(2,1)}), bf16[8,8,4096]{2,1,0:T(8,128)(2,1)}, u32[]{:S(2)}, u32[]{:S(2)}) %all-to-all-start.1) | async-done | bytes 524320 | tf_op jit(solution)/shard_map/all_to_all | solution.py:42
  163.0 2.1 %copy.24 = bf16[8,8,4096]{2,1,0:T(8,128)(2,1)} copy(bf16[8,8,4096]{2,0,1:T(8,128)(2,1)} %bitcast.12) | data formatting | bytes 1048576 | tf_op jit(solution)/shard_map/all_to_all | solution.py:42
  165.1 2.1 %reshape.51 = bf16[8,512,64]{2,1,0:T(8,128)(2,1)S(1)} reshape(bf16[8,8,4096]{2,1,0:T(8,128)(2,1)} %copy.24) | data formatting | bytes 1048576 | tf_op jit(solution)/shard_map/reshape | solution.py:60
  167.1 17.7 %all-reduce.3.cloned.1.call-done = bf16[8,128,64]{1,2,0:T(8,128)(2,1)} async-done(((bf16[8,128,64]{1,2,0:T(8,128)(2,1)}), bf16[8,128,64]{1,2,0:T(8,128)(2,1)}) %all-reduce.3.cloned.1.call-update) | async-done | bytes 131088 | tf_op jit(solution)/shard_map/psum | solution.py:65
  184.9 1.4 fusion.16
  186.3 1.4 fusion.14
  (35 shorter events, 3.8 us)
Async XLA Ops:
  6.5 107.1 %copy-start = (bf16[128,256]{1,0:T(8,128)(2,1)S(1)}, bf16[128,256]{1,0:T(8,128)(2,1)}, u32[]{:S(2)}) copy-start(bf16[128,256]{1,0:T(8,128)(2,1)} %param.21) | copy-start | bytes 196612
  6.5 39.6 %all-gather.3.cloned.1.call-start = ((), (), s32[]{:S(2)}) async-start(), calls=%async_computation.5 | async-start | bytes 5242880 | tf_op jit(solution)/shard_map/all_gather | solution.py:44
  7.3 142.8 %reduce-scatter.2.cloned.1.call-start = ((), (), s32[]{:S(2)}) async-start(), calls=%async_computation.3 | async-start | bytes 5242880 | tf_op jit(solution)/shard_map/reduce_scatter | solution.py:56
  46.1 3.4 %copy-start.1 = (bf16[4096,512]{1,0:T(8,128)(2,1)S(1)}, bf16[4096,512]{1,0:T(8,128)(2,1)}, u32[]{:S(2)}) copy-start(bf16[4096,512]{1,0:T(8,128)(2,1)} %all-gather.3.cloned.1.call-done) | copy-start | bytes 12582916
  66.6 2.1 %copy-start.2 = (bf16[1024,2048]{0,1:T(8,128)(2,1)}, bf16[1024,2048]{0,1:T(8,128)(2,1)S(1)}, u32[]{:S(2)}) copy-start(bf16[1024,2048]{0,1:T(8,128)(2,1)S(1)} %fusion.2) | copy-start | bytes 12582916
  78.7 21.3 %copy-start.5 = (f32[8,64]{1,0:T(8,128)S(1)}, f32[8,64]{1,0:T(8,128)}, u32[]{:S(2)}) copy-start(f32[8,64]{1,0:T(8,128)} %param.17) | copy-start | bytes 6148
  78.7 21.4 %copy-start.7 = (u32[32]{0:T(128)S(1)}, u32[32]{0:T(128)}, u32[]{:S(2)}) copy-start(u32[32]{0:T(128)} %constant.73) | copy-start | bytes 388
  78.7 23.4 %copy-start.6 = (s32[8]{0:T(128)S(1)}, s32[8]{0:T(128)}, u32[]{:S(2)}) copy-start(s32[8]{0:T(128)} %param.19) | copy-start | bytes 100
  125.7 18.7 %all-to-all-start = ((bf16[8,8,4096]{2,1,0:T(8,128)(2,1)}), bf16[8,8,4096]{2,1,0:T(8,128)(2,1)S(1)}, u32[]{:S(2)}, u32[]{:S(2)}) async-start(bf16[8,8,4096]{2,1,0:T(8,128)(2,1)} %fusion.12), calls=%async_computation.1 | async-start | bytes 1048576 | tf_op jit(solution)/shard_map/all_to_all | solution.py:41
  144.4 18.6 %all-to-all-start.1 = ((bf16[8,8,4096]{2,1,0:T(8,128)(2,1)}), bf16[8,8,4096]{2,1,0:T(8,128)(2,1)}, u32[]{:S(2)}, u32[]{:S(2)}) async-start(bf16[8,8,4096]{2,1,0:T(8,128)(2,1)} %fusion.13), calls=%async_computation.2 | async-start | bytes 1048576 | tf_op jit(solution)/shard_map/all_to_all | solution.py:42
  148.5 36.3 %all-reduce.3.cloned.1.call-start = ((), (), s32[]{:S(2)}) async-start(), calls=%async_computation.4 | async-start | bytes 262144 | tf_op jit(solution)/shard_map/psum | solution.py:65
  148.6 37.7 %copy-start.3 = (bf16[1024,512]{1,0:T(8,128)(2,1)S(1)}, bf16[1024,512]{1,0:T(8,128)(2,1)}, u32[]{:S(2)}) copy-start(bf16[1024,512]{1,0:T(8,128)(2,1)} %param.12) | copy-start | bytes 3145732
  150.1 36.2 %copy-start.4 = (bf16[1024,512]{1,0:T(8,128)(2,1)S(1)}, bf16[1024,512]{1,0:T(8,128)(2,1)}, u32[]{:S(2)}) copy-start(bf16[1024,512]{1,0:T(8,128)(2,1)} %reduce-scatter.2.cloned.1.call-done) | copy-start | bytes 3145732
Sparse Core Ops, SparseCore 0:
  8.9 37.1 all-gather.2
  99.4 44.3 reduce-scatter.1
  152.7 32.1 all-reduce.2
